TPU v7x, 32 devices: a whole 2x2x4 slice. The times are simulated.
32 devices in a mesh: row: 4 (over z), col: 8 (over y, x, core).
Axes of the slice: x: 2, y: 2, z: 4, core: 2. Of those that a mesh axis runs over, the one named last changes fastest.
Arguments:
- adjacency: int32 [32768, 2048], P('col', 'row'), may hold values from -2147483648 to 2147483647, as said below
- frontier: bfloat16 [65536, 128], P(('row', 'col')), may hold values from 0 to 1, as said below
- visited: int32 [4, 32768], P(None, ('col', 'row')), may hold values from -2147483648 to 2147483647, as said below
Outputs:
- path_counts: float32 [32768, 128], P(('col', 'row'))
- reached_bits: int32 [4, 32768], P(None, ('col', 'row'))
Inputs may be any that keep to these rules, and one draw needn't show every extreme that they name: Bit k of adjacency[d, w] is the edge from source vertex 32 w + k to destination d; degrees and edge densities differ between vertices and between blocks of 128 by 128 vertices. `frontier`: values are zero or between 0.1 and 1. Bit k of visited[w, d] tells whether destination d was reached from root 32 w + k.
All inputs are finite; a program needn't handle non-finite values.
Results may differ from a plain program's by a relative error of at most 0.0003.
Values may be sent and summed in bfloat16 or wider, within the bound.
A program may use at most 64 MiB of HBM per device.

v0:
```python
import functools
import math

import jax
import jax.numpy as jnp
from jax import lax
from jax.sharding import PartitionSpec as P


def expand_bits(packed):
    shift_table = jnp.arange(32, dtype=jnp.int32)
    bit_table = jnp.bitwise_and(jnp.right_shift(packed[:, :, None], shift_table), 1)
    return bit_table.reshape(packed.shape[0], packed.shape[1] * 32).astype(jnp.bfloat16)


def tile_product(packed, vectors):
    row_total = packed.shape[0]
    src_width = vectors.shape[0]
    row_len = math.gcd(row_total, 1024)
    block_len = math.gcd(src_width, 4096)
    block_count = src_width // block_len
    row_blocks = packed.reshape(row_total // row_len, row_len, packed.shape[1])

    def one_rows(packed_rows):
        initial = jnp.zeros((row_len, vectors.shape[1]), jnp.float32)

        def add_block(turn_index, total):
            offset = turn_index * block_len
            packed_cols = lax.dynamic_slice_in_dim(packed_rows, offset // 32, block_len // 32, 1)
            vector_rows = lax.dynamic_slice_in_dim(vectors, offset, block_len, 0)
            return total + jnp.dot(
                expand_bits(packed_cols), vector_rows, preferred_element_type=jnp.float32
            )

        return lax.fori_loop(0, block_count, add_block, initial)

    return lax.map(one_rows, row_blocks).reshape(row_total, vectors.shape[1])


def finish(reached, visited):
    row_count = reached.shape[0]
    word_count = visited.shape[0]
    shift_table = jnp.arange(32, dtype=jnp.int32)
    seen_bits = jnp.bitwise_and(jnp.right_shift(visited[:, :, None], shift_table), 1)
    seen_bits = jnp.transpose(seen_bits, (1, 0, 2)).reshape(row_count, word_count * 32)
    path_counts = jnp.where(seen_bits == 1, jnp.float32(0.0), reached)
    fresh = jnp.logical_and(seen_bits == 0, reached > 0).astype(jnp.int32)
    fresh = fresh.reshape(row_count, word_count, 32)
    added = functools.reduce(
        jnp.bitwise_or, [jnp.left_shift(fresh[:, :, position], position) for position in range(32)]
    )
    reached_bits = jnp.bitwise_or(visited, jnp.transpose(added))
    return (path_counts, reached_bits)


def shards(adjacency, frontier, visited):
    partial_sum = tile_product(adjacency, lax.all_gather(frontier, "col", axis=0, tiled=True))
    reached = lax.psum_scatter(partial_sum, "row", scatter_dimension=0, tiled=True)
    return finish(reached, visited)


def solution(mesh):
    placed = (P("col", "row"), P(("row", "col"), None), P(None, ("col", "row")))
    return jax.shard_map(
        shards,
        mesh=mesh,
        in_specs=placed,
        out_specs=(P(("col", "row"), None), P(None, ("col", "row"))),
        check_vma=False,
    )
```

profile of v0, /device:TPU:9, one launch (start us, length us, event | category | flops | bytes accessed | tf_op | source)
XLA Modules:
  0.0 299.1 jit_solution(3641786768029354774)
XLA Ops:
  7.2 0.7 all-gather.2.cloned.1.call-update
  8.0 40.1 %all-gather.2.cloned.1.call-done = bf16[16384,128]{1,0:T(8,128)(2,1)} async-done(((bf16[2048,128]{1,0:T(8,128)(2,1)}), bf16[16384,128]{1,0:T(8,128)(2,1)}) %all-gather.2.cloned.1.call-update) | async-done | bytes 4194320 | tf_op jit(solution)/shard_map/all_gather | solution.py:57
  48.0 195.2 %while.36 = (s32[]{:T(128)}, f32[4,1024,128]{2,1,0:T(8,128)}, s32[4,1024,512]{2,1,0:T(8,128)}, bf16[16384,128]{1,0:T(8,128)(2,1)}, s32[]{:T(128)}, /*index=5*/s3...) while((s32[]{:T(128)}, f32[4,1024,128]{2,1,0:T(8,128)}, ...), condition=%wide.region_3.4_spmd, body=%wide.region_0.3_spmd.sunk | while | flops 1086586880 | bytes 29951060 | solution.py:37
  48.0 3.1 %constant_dynamic-slice_fusion.4 = s32[1,1024,512]{2,1,0:T(8,128)} fusion(s32[4,1024,512]{2,1,0:T(8,128)} %get-tuple-element.379, s32[]{:T(128)} %get-tuple-element.363), kind=kLoop, calls=%fused_computation.8.clone.1 | loop fusion | bytes 4194308 | tf_op jit(solution)/shard_map/while/body/jit(dynamic_index_in_dim)/dynamic_slice | solution.py:37
  51.2 1.9 copy.298
  53.1 42.9 %while.37 = (s32[]{:T(128)}, f32[1024,128]{1,0:T(8,128)S(1)}, s32[1024,512]{0,1:T(8,128)S(1)}, bf16[16384,128]{1,0:T(8,128)(2,1)}, s32[]{:T(128)}, /*index=5*/s3...) while((s32[]{:T(128)}, f32[1024,128]{1,0:T(8,128)S(1)}, ...), condition=%wide.region_2.2_spmd.clone, body=%wide.region_1.1_spmd.clone.sunk | while | flops 1086586880 | bytes 20513124 | solution.py:35
  53.3 4.4 %fusion.66 = bf16[1024,4096]{0,1:T(8,128)(2,1)} fusion(s32[4096]{0:T(1024)S(1)} %shift_right_arithmetic.108, s32[1024,128]{0,1:T(8,128)S(1)} %constant_dynamic-slice_fusion.5), kind=kLoop, calls=%fused_computation.2.clone.1 | loop fusion | flops 12582912 | bytes 8929280 | tf_op jit(solution)/shard_map/while/body/eval_jaxpr/while/body/eval_jaxpr/convert_element_type | solution.py:13
  57.7 6.1 %convolution_add_fusion.2 = f32[1024,128]{1,0:T(8,128)S(1)} fusion(bf16[1024,4096]{0,1:T(8,128)(2,1)} %fusion.66, bf16[16384,128]{1,0:T(8,128)(2,1)} %get-tuple-element.340, s32[]{:T(128)S(6)} %select_n.46, f32[1024,128]{1,0:T(8,128)S(1)} %get-tuple-element.326, pred[]{:T(512)S(6)} %compare.13), kind=kOutput, calls=%fused_computation.3.clone.1 | convolution fusion | flops 1074003968 | bytes 10485765 | tf_op jit(solution)/shard_map/while/body/eval_jaxpr/while/body/eval_jaxpr/dot_general | solution.py:31
  63.9 0.1 shift_right_arithmetic.108
  64.0 4.4 %fusion.66 = bf16[1024,4096]{0,1:T(8,128)(2,1)} fusion(s32[4096]{0:T(1024)S(1)} %shift_right_arithmetic.108, s32[1024,128]{0,1:T(8,128)S(1)} %constant_dynamic-slice_fusion.5), kind=kLoop, calls=%fused_computation.2.clone.1 | loop fusion | flops 12582912 | bytes 8929280 | tf_op jit(solution)/shard_map/while/body/eval_jaxpr/while/body/eval_jaxpr/convert_element_type | solution.py:13
  68.4 6.1 %convolution_add_fusion.2 = f32[1024,128]{1,0:T(8,128)S(1)} fusion(bf16[1024,4096]{0,1:T(8,128)(2,1)} %fusion.66, bf16[16384,128]{1,0:T(8,128)(2,1)} %get-tuple-element.340, s32[]{:T(128)S(6)} %select_n.46, f32[1024,128]{1,0:T(8,128)S(1)} %get-tuple-element.326, pred[]{:T(512)S(6)} %compare.13), kind=kOutput, calls=%fused_computation.3.clone.1 | convolution fusion | flops 1074003968 | bytes 10485765 | tf_op jit(solution)/shard_map/while/body/eval_jaxpr/while/body/eval_jaxpr/dot_general | solution.py:31
  74.7 0.1 shift_right_arithmetic.108
  74.7 4.4 %fusion.66 = bf16[1024,4096]{0,1:T(8,128)(2,1)} fusion(s32[4096]{0:T(1024)S(1)} %shift_right_arithmetic.108, s32[1024,128]{0,1:T(8,128)S(1)} %constant_dynamic-slice_fusion.5), kind=kLoop, calls=%fused_computation.2.clone.1 | loop fusion | flops 12582912 | bytes 8929280 | tf_op jit(solution)/shard_map/while/body/eval_jaxpr/while/body/eval_jaxpr/convert_element_type | solution.py:13
  79.2 6.1 %convolution_add_fusion.2 = f32[1024,128]{1,0:T(8,128)S(1)} fusion(bf16[1024,4096]{0,1:T(8,128)(2,1)} %fusion.66, bf16[16384,128]{1,0:T(8,128)(2,1)} %get-tuple-element.340, s32[]{:T(128)S(6)} %select_n.46, f32[1024,128]{1,0:T(8,128)S(1)} %get-tuple-element.326, pred[]{:T(512)S(6)} %compare.13), kind=kOutput, calls=%fused_computation.3.clone.1 | convolution fusion | flops 1074003968 | bytes 10485765 | tf_op jit(solution)/shard_map/while/body/eval_jaxpr/while/body/eval_jaxpr/dot_general | solution.py:31
  85.4 0.1 shift_right_arithmetic.108
  85.5 4.4 %fusion.66 = bf16[1024,4096]{0,1:T(8,128)(2,1)} fusion(s32[4096]{0:T(1024)S(1)} %shift_right_arithmetic.108, s32[1024,128]{0,1:T(8,128)S(1)} %constant_dynamic-slice_fusion.5), kind=kLoop, calls=%fused_computation.2.clone.1 | loop fusion | flops 12582912 | bytes 8929280 | tf_op jit(solution)/shard_map/while/body/eval_jaxpr/while/body/eval_jaxpr/convert_element_type | solution.py:13
  89.9 6.1 %convolution_add_fusion.2 = f32[1024,128]{1,0:T(8,128)S(1)} fusion(bf16[1024,4096]{0,1:T(8,128)(2,1)} %fusion.66, bf16[16384,128]{1,0:T(8,128)(2,1)} %get-tuple-element.340, s32[]{:T(128)S(6)} %select_n.46, f32[1024,128]{1,0:T(8,128)S(1)} %get-tuple-element.326, pred[]{:T(512)S(6)} %compare.13), kind=kOutput, calls=%fused_computation.3.clone.1 | convolution fusion | flops 1074003968 | bytes 10485765 | tf_op jit(solution)/shard_map/while/body/eval_jaxpr/while/body/eval_jaxpr/dot_general | solution.py:31
  96.0 0.9 bitcast_dynamic-update-slice_fusion.2
  96.9 3.1 %constant_dynamic-slice_fusion.4 = s32[1,1024,512]{2,1,0:T(8,128)} fusion(s32[4,1024,512]{2,1,0:T(8,128)} %get-tuple-element.379, s32[]{:T(128)} %get-tuple-element.363), kind=kLoop, calls=%fused_computation.8.clone.1 | loop fusion | bytes 4194308 | tf_op jit(solution)/shard_map/while/body/jit(dynamic_index_in_dim)/dynamic_slice | solution.py:37
  100.0 1.9 copy.298
  101.9 42.9 %while.37 = (s32[]{:T(128)}, f32[1024,128]{1,0:T(8,128)S(1)}, s32[1024,512]{0,1:T(8,128)S(1)}, bf16[16384,128]{1,0:T(8,128)(2,1)}, s32[]{:T(128)}, /*index=5*/s3...) while((s32[]{:T(128)}, f32[1024,128]{1,0:T(8,128)S(1)}, ...), condition=%wide.region_2.2_spmd.clone, body=%wide.region_1.1_spmd.clone.sunk | while | flops 1086586880 | bytes 20513124 | solution.py:35
  102.0 0.1 shift_right_arithmetic.108
  102.1 4.4 %fusion.66 = bf16[1024,4096]{0,1:T(8,128)(2,1)} fusion(s32[4096]{0:T(1024)S(1)} %shift_right_arithmetic.108, s32[1024,128]{0,1:T(8,128)S(1)} %constant_dynamic-slice_fusion.5), kind=kLoop, calls=%fused_computation.2.clone.1 | loop fusion | flops 12582912 | bytes 8929280 | tf_op jit(solution)/shard_map/while/body/eval_jaxpr/while/body/eval_jaxpr/convert_element_type | solution.py:13
  106.5 6.1 %convolution_add_fusion.2 = f32[1024,128]{1,0:T(8,128)S(1)} fusion(bf16[1024,4096]{0,1:T(8,128)(2,1)} %fusion.66, bf16[16384,128]{1,0:T(8,128)(2,1)} %get-tuple-element.340, s32[]{:T(128)S(6)} %select_n.46, f32[1024,128]{1,0:T(8,128)S(1)} %get-tuple-element.326, pred[]{:T(512)S(6)} %compare.13), kind=kOutput, calls=%fused_computation.3.clone.1 | convolution fusion | flops 1074003968 | bytes 10485765 | tf_op jit(solution)/shard_map/while/body/eval_jaxpr/while/body/eval_jaxpr/dot_general | solution.py:31
  112.8 4.4 %fusion.66 = bf16[1024,4096]{0,1:T(8,128)(2,1)} fusion(s32[4096]{0:T(1024)S(1)} %shift_right_arithmetic.108, s32[1024,128]{0,1:T(8,128)S(1)} %constant_dynamic-slice_fusion.5), kind=kLoop, calls=%fused_computation.2.clone.1 | loop fusion | flops 12582912 | bytes 8929280 | tf_op jit(solution)/shard_map/while/body/eval_jaxpr/while/body/eval_jaxpr/convert_element_type | solution.py:13
  117.3 6.1 %convolution_add_fusion.2 = f32[1024,128]{1,0:T(8,128)S(1)} fusion(bf16[1024,4096]{0,1:T(8,128)(2,1)} %fusion.66, bf16[16384,128]{1,0:T(8,128)(2,1)} %get-tuple-element.340, s32[]{:T(128)S(6)} %select_n.46, f32[1024,128]{1,0:T(8,128)S(1)} %get-tuple-element.326, pred[]{:T(512)S(6)} %compare.13), kind=kOutput, calls=%fused_computation.3.clone.1 | convolution fusion | flops 1074003968 | bytes 10485765 | tf_op jit(solution)/shard_map/while/body/eval_jaxpr/while/body/eval_jaxpr/dot_general | solution.py:31
  123.6 4.4 %fusion.66 = bf16[1024,4096]{0,1:T(8,128)(2,1)} fusion(s32[4096]{0:T(1024)S(1)} %shift_right_arithmetic.108, s32[1024,128]{0,1:T(8,128)S(1)} %constant_dynamic-slice_fusion.5), kind=kLoop, calls=%fused_computation.2.clone.1 | loop fusion | flops 12582912 | bytes 8929280 | tf_op jit(solution)/shard_map/while/body/eval_jaxpr/while/body/eval_jaxpr/convert_element_type | solution.py:13
  128.0 6.1 %convolution_add_fusion.2 = f32[1024,128]{1,0:T(8,128)S(1)} fusion(bf16[1024,4096]{0,1:T(8,128)(2,1)} %fusion.66, bf16[16384,128]{1,0:T(8,128)(2,1)} %get-tuple-element.340, s32[]{:T(128)S(6)} %select_n.46, f32[1024,128]{1,0:T(8,128)S(1)} %get-tuple-element.326, pred[]{:T(512)S(6)} %compare.13), kind=kOutput, calls=%fused_computation.3.clone.1 | convolution fusion | flops 1074003968 | bytes 10485765 | tf_op jit(solution)/shard_map/while/body/eval_jaxpr/while/body/eval_jaxpr/dot_general | solution.py:31
  134.3 4.4 %fusion.66 = bf16[1024,4096]{0,1:T(8,128)(2,1)} fusion(s32[4096]{0:T(1024)S(1)} %shift_right_arithmetic.108, s32[1024,128]{0,1:T(8,128)S(1)} %constant_dynamic-slice_fusion.5), kind=kLoop, calls=%fused_computation.2.clone.1 | loop fusion | flops 12582912 | bytes 8929280 | tf_op jit(solution)/shard_map/while/body/eval_jaxpr/while/body/eval_jaxpr/convert_element_type | solution.py:13
  138.7 6.1 %convolution_add_fusion.2 = f32[1024,128]{1,0:T(8,128)S(1)} fusion(bf16[1024,4096]{0,1:T(8,128)(2,1)} %fusion.66, bf16[16384,128]{1,0:T(8,128)(2,1)} %get-tuple-element.340, s32[]{:T(128)S(6)} %select_n.46, f32[1024,128]{1,0:T(8,128)S(1)} %get-tuple-element.326, pred[]{:T(512)S(6)} %compare.13), kind=kOutput, calls=%fused_computation.3.clone.1 | convolution fusion | flops 1074003968 | bytes 10485765 | tf_op jit(solution)/shard_map/while/body/eval_jaxpr/while/body/eval_jaxpr/dot_general | solution.py:31
  144.8 0.9 bitcast_dynamic-update-slice_fusion.2
  145.7 3.1 %constant_dynamic-slice_fusion.4 = s32[1,1024,512]{2,1,0:T(8,128)} fusion(s32[4,1024,512]{2,1,0:T(8,128)} %get-tuple-element.379, s32[]{:T(128)} %get-tuple-element.363), kind=kLoop, calls=%fused_computation.8.clone.1 | loop fusion | bytes 4194308 | tf_op jit(solution)/shard_map/while/body/jit(dynamic_index_in_dim)/dynamic_slice | solution.py:37
  148.8 1.9 copy.298
  150.7 42.9 %while.37 = (s32[]{:T(128)}, f32[1024,128]{1,0:T(8,128)S(1)}, s32[1024,512]{0,1:T(8,128)S(1)}, bf16[16384,128]{1,0:T(8,128)(2,1)}, s32[]{:T(128)}, /*index=5*/s3...) while((s32[]{:T(128)}, f32[1024,128]{1,0:T(8,128)S(1)}, ...), condition=%wide.region_2.2_spmd.clone, body=%wide.region_1.1_spmd.clone.sunk | while | flops 1086586880 | bytes 20513124 | solution.py:35
  150.9 4.4 %fusion.66 = bf16[1024,4096]{0,1:T(8,128)(2,1)} fusion(s32[4096]{0:T(1024)S(1)} %shift_right_arithmetic.108, s32[1024,128]{0,1:T(8,128)S(1)} %constant_dynamic-slice_fusion.5), kind=kLoop, calls=%fused_computation.2.clone.1 | loop fusion | flops 12582912 | bytes 8929280 | tf_op jit(solution)/shard_map/while/body/eval_jaxpr/while/body/eval_jaxpr/convert_element_type | solution.py:13
  155.4 6.1 %convolution_add_fusion.2 = f32[1024,128]{1,0:T(8,128)S(1)} fusion(bf16[1024,4096]{0,1:T(8,128)(2,1)} %fusion.66, bf16[16384,128]{1,0:T(8,128)(2,1)} %get-tuple-element.340, s32[]{:T(128)S(6)} %select_n.46, f32[1024,128]{1,0:T(8,128)S(1)} %get-tuple-element.326, pred[]{:T(512)S(6)} %compare.13), kind=kOutput, calls=%fused_computation.3.clone.1 | convolution fusion | flops 1074003968 | bytes 10485765 | tf_op jit(solution)/shard_map/while/body/eval_jaxpr/while/body/eval_jaxpr/dot_general | solution.py:31
  161.7 4.4 %fusion.66 = bf16[1024,4096]{0,1:T(8,128)(2,1)} fusion(s32[4096]{0:T(1024)S(1)} %shift_right_arithmetic.108, s32[1024,128]{0,1:T(8,128)S(1)} %constant_dynamic-slice_fusion.5), kind=kLoop, calls=%fused_computation.2.clone.1 | loop fusion | flops 12582912 | bytes 8929280 | tf_op jit(solution)/shard_map/while/body/eval_jaxpr/while/body/eval_jaxpr/convert_element_type | solution.py:13
  166.1 6.1 %convolution_add_fusion.2 = f32[1024,128]{1,0:T(8,128)S(1)} fusion(bf16[1024,4096]{0,1:T(8,128)(2,1)} %fusion.66, bf16[16384,128]{1,0:T(8,128)(2,1)} %get-tuple-element.340, s32[]{:T(128)S(6)} %select_n.46, f32[1024,128]{1,0:T(8,128)S(1)} %get-tuple-element.326, pred[]{:T(512)S(6)} %compare.13), kind=kOutput, calls=%fused_computation.3.clone.1 | convolution fusion | flops 1074003968 | bytes 10485765 | tf_op jit(solution)/shard_map/while/body/eval_jaxpr/while/body/eval_jaxpr/dot_general | solution.py:31
  172.4 4.4 %fusion.66 = bf16[1024,4096]{0,1:T(8,128)(2,1)} fusion(s32[4096]{0:T(1024)S(1)} %shift_right_arithmetic.108, s32[1024,128]{0,1:T(8,128)S(1)} %constant_dynamic-slice_fusion.5), kind=kLoop, calls=%fused_computation.2.clone.1 | loop fusion | flops 12582912 | bytes 8929280 | tf_op jit(solution)/shard_map/while/body/eval_jaxpr/while/body/eval_jaxpr/convert_element_type | solution.py:13
  176.8 6.1 %convolution_add_fusion.2 = f32[1024,128]{1,0:T(8,128)S(1)} fusion(bf16[1024,4096]{0,1:T(8,128)(2,1)} %fusion.66, bf16[16384,128]{1,0:T(8,128)(2,1)} %get-tuple-element.340, s32[]{:T(128)S(6)} %select_n.46, f32[1024,128]{1,0:T(8,128)S(1)} %get-tuple-element.326, pred[]{:T(512)S(6)} %compare.13), kind=kOutput, calls=%fused_computation.3.clone.1 | convolution fusion | flops 1074003968 | bytes 10485765 | tf_op jit(solution)/shard_map/while/body/eval_jaxpr/while/body/eval_jaxpr/dot_general | solution.py:31
  183.1 4.4 %fusion.66 = bf16[1024,4096]{0,1:T(8,128)(2,1)} fusion(s32[4096]{0:T(1024)S(1)} %shift_right_arithmetic.108, s32[1024,128]{0,1:T(8,128)S(1)} %constant_dynamic-slice_fusion.5), kind=kLoop, calls=%fused_computation.2.clone.1 | loop fusion | flops 12582912 | bytes 8929280 | tf_op jit(solution)/shard_map/while/body/eval_jaxpr/while/body/eval_jaxpr/convert_element_type | solution.py:13
  187.6 6.1 %convolution_add_fusion.2 = f32[1024,128]{1,0:T(8,128)S(1)} fusion(bf16[1024,4096]{0,1:T(8,128)(2,1)} %fusion.66, bf16[16384,128]{1,0:T(8,128)(2,1)} %get-tuple-element.340, s32[]{:T(128)S(6)} %select_n.46, f32[1024,128]{1,0:T(8,128)S(1)} %get-tuple-element.326, pred[]{:T(512)S(6)} %compare.13), kind=kOutput, calls=%fused_computation.3.clone.1 | convolution fusion | flops 1074003968 | bytes 10485765 | tf_op jit(solution)/shard_map/while/body/eval_jaxpr/while/body/eval_jaxpr/dot_general | solution.py:31
  193.7 0.8 bitcast_dynamic-update-slice_fusion.2
  194.5 3.1 %constant_dynamic-slice_fusion.4 = s32[1,1024,512]{2,1,0:T(8,128)} fusion(s32[4,1024,512]{2,1,0:T(8,128)} %get-tuple-element.379, s32[]{:T(128)} %get-tuple-element.363), kind=kLoop, calls=%fused_computation.8.clone.1 | loop fusion | bytes 4194308 | tf_op jit(solution)/shard_map/while/body/jit(dynamic_index_in_dim)/dynamic_slice | solution.py:37
  197.6 1.9 copy.298
  199.5 42.9 %while.37 = (s32[]{:T(128)}, f32[1024,128]{1,0:T(8,128)S(1)}, s32[1024,512]{0,1:T(8,128)S(1)}, bf16[16384,128]{1,0:T(8,128)(2,1)}, s32[]{:T(128)}, /*index=5*/s3...) while((s32[]{:T(128)}, f32[1024,128]{1,0:T(8,128)S(1)}, ...), condition=%wide.region_2.2_spmd.clone, body=%wide.region_1.1_spmd.clone.sunk | while | flops 1086586880 | bytes 20513124 | solution.py:35
  199.7 4.4 %fusion.66 = bf16[1024,4096]{0,1:T(8,128)(2,1)} fusion(s32[4096]{0:T(1024)S(1)} %shift_right_arithmetic.108, s32[1024,128]{0,1:T(8,128)S(1)} %constant_dynamic-slice_fusion.5), kind=kLoop, calls=%fused_computation.2.clone.1 | loop fusion | flops 12582912 | bytes 8929280 | tf_op jit(solution)/shard_map/while/body/eval_jaxpr/while/body/eval_jaxpr/convert_element_type | solution.py:13
  204.2 6.1 %convolution_add_fusion.2 = f32[1024,128]{1,0:T(8,128)S(1)} fusion(bf16[1024,4096]{0,1:T(8,128)(2,1)} %fusion.66, bf16[16384,128]{1,0:T(8,128)(2,1)} %get-tuple-element.340, s32[]{:T(128)S(6)} %select_n.46, f32[1024,128]{1,0:T(8,128)S(1)} %get-tuple-element.326, pred[]{:T(512)S(6)} %compare.13), kind=kOutput, calls=%fused_computation.3.clone.1 | convolution fusion | flops 1074003968 | bytes 10485765 | tf_op jit(solution)/shard_map/while/body/eval_jaxpr/while/body/eval_jaxpr/dot_general | solution.py:31
  210.5 4.4 %fusion.66 = bf16[1024,4096]{0,1:T(8,128)(2,1)} fusion(s32[4096]{0:T(1024)S(1)} %shift_right_arithmetic.108, s32[1024,128]{0,1:T(8,128)S(1)} %constant_dynamic-slice_fusion.5), kind=kLoop, calls=%fused_computation.2.clone.1 | loop fusion | flops 12582912 | bytes 8929280 | tf_op jit(solution)/shard_map/while/body/eval_jaxpr/while/body/eval_jaxpr/convert_element_type | solution.py:13
  214.9 6.1 %convolution_add_fusion.2 = f32[1024,128]{1,0:T(8,128)S(1)} fusion(bf16[1024,4096]{0,1:T(8,128)(2,1)} %fusion.66, bf16[16384,128]{1,0:T(8,128)(2,1)} %get-tuple-element.340, s32[]{:T(128)S(6)} %select_n.46, f32[1024,128]{1,0:T(8,128)S(1)} %get-tuple-element.326, pred[]{:T(512)S(6)} %compare.13), kind=kOutput, calls=%fused_computation.3.clone.1 | convolution fusion | flops 1074003968 | bytes 10485765 | tf_op jit(solution)/shard_map/while/body/eval_jaxpr/while/body/eval_jaxpr/dot_general | solution.py:31
  221.2 4.4 %fusion.66 = bf16[1024,4096]{0,1:T(8,128)(2,1)} fusion(s32[4096]{0:T(1024)S(1)} %shift_right_arithmetic.108, s32[1024,128]{0,1:T(8,128)S(1)} %constant_dynamic-slice_fusion.5), kind=kLoop, calls=%fused_computation.2.clone.1 | loop fusion | flops 12582912 | bytes 8929280 | tf_op jit(solution)/shard_map/while/body/eval_jaxpr/while/body/eval_jaxpr/convert_element_type | solution.py:13
  225.6 6.1 %convolution_add_fusion.2 = f32[1024,128]{1,0:T(8,128)S(1)} fusion(bf16[1024,4096]{0,1:T(8,128)(2,1)} %fusion.66, bf16[16384,128]{1,0:T(8,128)(2,1)} %get-tuple-element.340, s32[]{:T(128)S(6)} %select_n.46, f32[1024,128]{1,0:T(8,128)S(1)} %get-tuple-element.326, pred[]{:T(512)S(6)} %compare.13), kind=kOutput, calls=%fused_computation.3.clone.1 | convolution fusion | flops 1074003968 | bytes 10485765 | tf_op jit(solution)/shard_map/while/body/eval_jaxpr/while/body/eval_jaxpr/dot_general | solution.py:31
  231.9 4.4 %fusion.66 = bf16[1024,4096]{0,1:T(8,128)(2,1)} fusion(s32[4096]{0:T(1024)S(1)} %shift_right_arithmetic.108, s32[1024,128]{0,1:T(8,128)S(1)} %constant_dynamic-slice_fusion.5), kind=kLoop, calls=%fused_computation.2.clone.1 | loop fusion | flops 12582912 | bytes 8929280 | tf_op jit(solution)/shard_map/while/body/eval_jaxpr/while/body/eval_jaxpr/convert_element_type | solution.py:13
  236.4 6.1 %convolution_add_fusion.2 = f32[1024,128]{1,0:T(8,128)S(1)} fusion(bf16[1024,4096]{0,1:T(8,128)(2,1)} %fusion.66, bf16[16384,128]{1,0:T(8,128)(2,1)} %get-tuple-element.340, s32[]{:T(128)S(6)} %select_n.46, f32[1024,128]{1,0:T(8,128)S(1)} %get-tuple-element.326, pred[]{:T(512)S(6)} %compare.13), kind=kOutput, calls=%fused_computation.3.clone.1 | convolution fusion | flops 1074003968 | bytes 10485765 | tf_op jit(solution)/shard_map/while/body/eval_jaxpr/while/body/eval_jaxpr/dot_general | solution.py:31
  242.5 0.8 bitcast_dynamic-update-slice_fusion.2
  243.3 3.0 copy.73
  246.3 0.1 shift_right_arithmetic.66
  246.4 41.3 %reduce-scatter.2.cloned.1.call-done = f32[1024,128]{0,1:T(8,128)} async-done(((f32[4096,128]{0,1:T(8,128)}), f32[1024,128]{0,1:T(8,128)}) %reduce-scatter.2.cloned.1.call-update) | async-done | bytes 524304 | tf_op jit(solution)/shard_map/reduce_scatter | solution.py:58
  287.7 1.2 fusion.9
  288.9 0.3 slice_shift-left_fusion
  289.2 0.2 fusion.59
  289.3 1.2 fusion.7
  290.5 1.0 copy.72
  291.5 0.7 fusion.14
  (55 shorter events, 2.1 us)
Async XLA Ops:
  7.2 40.9 %all-gather.2.cloned.1.call-start = ((), (), s32[]{:S(2)}) async-start(), calls=%async_computation.1 | async-start | bytes 4718592 | tf_op jit(solution)/shard_map/all_gather | solution.py:57
  7.9 279.8 %reduce-scatter.2.cloned.1.call-start = ((), (), s32[]{:S(2)}) async-start(), calls=%async_computation.2 | async-start | bytes 2621440 | tf_op jit(solution)/shard_map/reduce_scatter | solution.py:58
  243.3 44.4 %copy-start = (s32[4,1024]{1,0:T(4,128)S(1)}, s32[4,1024]{1,0:T(4,128)}, u32[]{:S(2)}) copy-start(s32[4,1024]{1,0:T(4,128)} %param.9) | copy-start | bytes 49156
Sparse Core Ops, SparseCore 0:
  9.9 38.1 all-gather.1
  246.4 41.2 reduce-scatter.1
where the time goes:
time: 303 us; the launch traced here: 299 us
  matrix products  97.5 us (32%)
  waiting for transfers between devices  82.1 us (27%)
  other arithmetic  74.2 us (24%)
  local copies, waits for them, and re-layouts  30 us (10%)
  between operations  14.1 us (5%)
    dot_general x16, matrix products, add_block(): jnp.dot(expand_bits(packed_cols), vector_rows, preferred_element_type=jnp...  97.5 us
    convert_element_type x16, other arithmetic, expand_bits(): bit_table.reshape(packed.shape[0], packed.shape[1] * 32)  70.8 us
    reduce_scatter x1, waiting for transfers between devices, shards(): lax.psum_scatter(partial_sum, 'row', scatter_dimension=0, tiled=True)  41.3 us
    all_gather x1, waiting for transfers between devices, shards(): lax.all_gather(frontier, 'col', axis=0, tiled=True)  40.1 us
    dynamic_slice x8, local copies, waits for them, and re-layouts, tile_product(): return lax.map(one_rows, row_blocks).reshape(row_total, vectors.shape[1])  20.1 us
  transfers between devices with their start and end apart: 2, of which 2 were waited for; matrix products, arithmetic and copies ran while one was open for 0% of the time, Pallas kernels for 0%

commit v1 on v0

v1 whole, which is shorter than its diff:
```python
import functools
import math

import jax
import jax.numpy as jnp
import numpy as np
from jax import lax
from jax.experimental import pallas as pl
from jax.experimental.pallas import tpu as pltpu
from jax.sharding import PartitionSpec as P

MESH = pl.DeviceIdType.MESH
LOW = 0.09
LEVELS = 65000.0


def expand_bits(words):
    one = jnp.full(words.shape, 1, jnp.float8_e4m3fn)
    zero = jnp.full(words.shape, 0, jnp.float8_e4m3fn)
    pieces = []
    for byte in range(4):
        part = (words >> (8 * byte)).astype(jnp.int8)
        for bit in range(8):
            mask = np.int8(-128) if bit == 7 else np.int8(1 << bit)
            pieces.append(jnp.where((part & mask) != 0, one, zero))
    return jnp.concatenate(pieces, axis=0)


def encode(value, scale):
    code = jnp.log(jnp.maximum(value, LOW)) * scale + (1.5 - math.log(LOW) * scale)
    code = jnp.where(value > 0, code, 0.0).astype(jnp.int32)
    return (code - 32768).astype(jnp.int16)


def decode(code, scale):
    code = code.astype(jnp.int32) + 32768
    value = jnp.exp((code - 1).astype(jnp.float32) * (1.0 / scale) + math.log(LOW))
    return jnp.where(code > 0, value, 0.0)


def flip(index, bit):
    return index + bit - 2 * bit * ((index // bit) % 2)


def kernel(
    n_row, n_col, adj, ft, visited, counts, bits,
    stage, words, fbuf, total, out_code, in_code,
    load_sem, own_sem, fsend, frecv, psend, precv,
):
    r, c = lax.axis_index("row"), lax.axis_index("col")
    dst, width = adj.shape
    depth = ft.shape[1]
    wide = width // n_col
    part = dst // n_row
    half = math.gcd(dst, 2048)
    halves = dst // half
    tile = stage.shape[1]
    tiles = dst // tile
    paired = n_col == 8
    scale = LEVELS / math.log(width * 32 * 1.01 / LOW)

    def load(t, slot):
        return pltpu.make_async_copy(
            adj.at[pl.ds(pl.multiple_of(t * tile, tile), tile), :], stage.at[slot], load_sem.at[slot]
        )

    load(0, 0).start()
    own = pltpu.make_async_copy(ft, fbuf.at[c], own_sem)
    own.start()

    if paired:
        mates = [flip(c, 1), flip(c, 2), flip(c, 4)]
    else:
        mates = [lax.rem(c + i, n_col) for i in range(1, n_col)]
    others = [lax.rem(r + i, n_row) for i in range(1, n_row)]
    barrier = pltpu.get_barrier_semaphore()
    for mate in mates:
        pl.semaphore_signal(barrier, inc=1, device_id={"col": mate}, device_id_type=MESH)
    for other in others:
        pl.semaphore_signal(barrier, inc=1, device_id={"row": other}, device_id_type=MESH)
    pl.semaphore_wait(barrier, len(mates) + len(others))

    def send(src, dst_ref, role, mate):
        return pltpu.make_async_remote_copy(
            src_ref=src, dst_ref=dst_ref, send_sem=fsend.at[role], recv_sem=frecv.at[role],
            device_id={"col": mate}, device_id_type=MESH,
        )

    if paired:
        pair, east, north = mates
        first, second = pl.ds(0, ft.shape[0] // 2), pl.ds(ft.shape[0] // 2, ft.shape[0] // 2)
        diagonal = flip(east, 4)
        slots = [pair, east, north, diagonal, diagonal, flip(pair, 2), flip(pair, 4), flip(diagonal, 1)]
        sends = [
            send(ft, fbuf.at[c], 0, pair),
            send(ft, fbuf.at[c], 1, east),
            send(ft, fbuf.at[c], 2, north),
            send(fbuf.at[east, first], fbuf.at[east, first], 3, north),
            send(fbuf.at[north, second], fbuf.at[north, second], 4, east),
            send(fbuf.at[east], fbuf.at[east], 5, pair),
            send(fbuf.at[north], fbuf.at[north], 6, pair),
            send(fbuf.at[diagonal], fbuf.at[diagonal], 7, pair),
        ]
        for role in (1, 2, 0):
            sends[role].start()

        def arrived(role):
            place = fbuf.at[slots[role]]
            if role == 3:
                place = fbuf.at[diagonal, first]
            if role == 4:
                place = fbuf.at[diagonal, second]
            send(place, place, role, pair).wait_recv()

    else:
        sends = [send(ft, fbuf.at[c], i, mate) for i, mate in enumerate(mates)]
        for copy in sends:
            copy.start()

    @pl.loop(0, tiles)
    def _(t):
        slot = lax.rem(t, 2)

        @pl.when(t + 1 < tiles)
        def _():
            load(t + 1, 1 - slot).start()

        load(t, slot).wait()
        words[:, pl.ds(pl.multiple_of(t * tile, tile), tile)] = stage[slot].T

    total[...] = jnp.zeros_like(total)
    own.wait()

    def product(slot, start, size):
        packed = words[pl.ds(pl.multiple_of(slot * wide, wide), wide), pl.ds(start, size)]
        return lax.dot_general(
            fbuf[slot], expand_bits(packed), (((1,), (0,)), ((), ())), preferred_element_type=jnp.float32
        )

    early = n_col - 2

    @pl.loop(0, early * halves)
    def _(t):
        step = t // halves
        start = pl.multiple_of(lax.rem(t, halves) * half, half)
        fresh = lax.rem(t, halves) == 0
        if paired:

            @pl.when(jnp.logical_and(fresh, step == 1))
            def _():
                arrived(0)

            @pl.when(jnp.logical_and(fresh, step == 2))
            def _():
                arrived(1)
                sends[3].start()
                sends[5].start()
                arrived(2)
                sends[4].start()
                sends[6].start()

            @pl.when(jnp.logical_and(fresh, step == 4))
            def _():
                arrived(5)

            @pl.when(jnp.logical_and(fresh, step == 5))
            def _():
                arrived(6)
                arrived(3)
                arrived(4)
                sends[7].start()

            slot = c
            for number, choice in enumerate((slots[0], slots[1], slots[2], slots[5], slots[6])):
                slot = jnp.where(step == number + 1, choice, slot)
        else:
            slot = lax.rem(c + n_col - step, n_col)

            @pl.when(jnp.logical_and(fresh, step > 0))
            def _():
                send(fbuf.at[slot], fbuf.at[slot], step - 1, mates[0]).wait_recv()

        total[:, pl.ds(start, half)] += product(slot, start, half)

    if paired:
        arrived(7)
        last = (slots[3], slots[7])
    else:
        last = (lax.rem(c + 2, n_col), lax.rem(c + 1, n_col))
        for slot, role in zip(last, (n_col - 3, n_col - 2)):
            send(fbuf.at[slot], fbuf.at[slot], role, mates[0]).wait_recv()

    def exchange(t, other):
        return pltpu.make_async_remote_copy(
            src_ref=out_code.at[t], dst_ref=in_code.at[t], send_sem=psend.at[t], recv_sem=precv.at[t],
            device_id={"row": other}, device_id_type=MESH,
        )

    @pl.loop(0, n_row)
    def _(t):
        other = lax.rem(r + 1 + t, n_row)
        start = pl.multiple_of(other * part, part)
        block = total[:, pl.ds(start, part)] + product(last[0], start, part)
        block = block + product(last[1], start, part)

        @pl.when(t < n_row - 1)
        def _():
            out_code[t] = encode(block, scale)
            exchange(t, other).start()

        @pl.when(t == n_row - 1)
        def _():
            total[:, pl.ds(0, part)] = block

    def received(t, value):
        exchange(t, others[0]).wait_recv()
        return value + decode(in_code[t], scale)

    reached = total[:, pl.ds(0, part)]
    for t in range(n_row - 1):
        reached = received(t, reached)
    place = lax.broadcasted_iota(jnp.int32, (32, part), 0)
    kept, added = [], []
    for word in range(visited.shape[0]):
        value = reached[word * 32 : word * 32 + 32]
        unseen = ((visited[word : word + 1, :] >> place) & 1) == 0
        kept.append(jnp.where(unseen, value, 0.0))
        marks = jnp.where(jnp.logical_and(unseen, value > 0), jnp.int32(1) << place, 0)
        added.append(jnp.sum(marks, axis=0, keepdims=True))
    counts[...] = jnp.concatenate(kept, axis=0).T
    bits[...] = visited[...] | jnp.concatenate(added, axis=0)
    for copy in sends:
        copy.wait_send()
    for t in range(n_row - 1):
        exchange(t, others[0]).wait_send()


def shards(n_row, n_col, adjacency, frontier, visited):
    dst, width = adjacency.shape
    depth, roots = frontier.shape
    part = dst // n_row
    tile = math.gcd(dst, 256)
    ft = jnp.transpose(frontier.reshape(depth // 32, 32, roots), (2, 1, 0)).reshape(roots, depth)
    vmem = pl.BlockSpec(memory_space=pltpu.VMEM)
    roles = 8 if n_col == 8 else n_col - 1
    dma = pltpu.SemaphoreType.DMA
    return pl.pallas_call(
        functools.partial(kernel, n_row, n_col),
        out_shape=(
            jax.ShapeDtypeStruct((part, roots), jnp.float32),
            jax.ShapeDtypeStruct((visited.shape[0], part), jnp.int32),
        ),
        in_specs=[pl.BlockSpec(memory_space=pl.ANY), vmem, vmem],
        out_specs=(vmem, vmem),
        scratch_shapes=[
            pltpu.VMEM((2, tile, width), jnp.int32),
            pltpu.VMEM((width, dst), jnp.int32),
            pltpu.VMEM((n_col, roots, depth), jnp.bfloat16),
            pltpu.VMEM((roots, dst), jnp.float32),
            pltpu.VMEM((n_row - 1, roots, part), jnp.int16),
            pltpu.VMEM((n_row - 1, roots, part), jnp.int16),
            dma((2,)),
            dma,
            dma((roles,)),
            dma((roles,)),
            dma((n_row - 1,)),
            dma((n_row - 1,)),
        ],
        compiler_params=pltpu.CompilerParams(
            collective_id=0, has_side_effects=True, vmem_limit_bytes=56 * 2**20
        ),
    )(adjacency, ft, visited)


def solution(mesh):
    placed = (P("col", "row"), P(("row", "col"), None), P(None, ("col", "row")))
    return jax.shard_map(
        functools.partial(shards, mesh.shape["row"], mesh.shape["col"]),
        mesh=mesh,
        in_specs=placed,
        out_specs=(P(("col", "row"), None), P(None, ("col", "row"))),
        check_vma=False,
    )
```

time: 303 us -> 63.2 us (0.21); the launches traced: 299 us -> 62.7 us
  matrix products: 97.5 us -> 0 us
  waiting for transfers between devices: 82.1 us -> 0 us
  other arithmetic: 74.2 us -> 0 us
  Pallas kernels: 0 us -> 56.6 us
  local copies, waits for them, and re-layouts: 30 us -> 5.45 us
  between operations: 14.1 us -> 0.64 us
    dot_general x16 -> x0, matrix products: 97.5 us -> none  [add_block(): jnp.dot(expand_bits(packed_cols), vector_rows, preferred_element_type=jnp...]
    convert_element_type x16 -> x0, other arithmetic: 70.8 us -> none  [expand_bits(): bit_table.reshape(packed.shape[0], packed.shape[1] * 32)]
    pallas_call x0 -> x1, Pallas kernels: none -> 56.6 us  [shards(): pl.pallas_call(functools.partial(kernel, n_row, n_col), out_shape=(jax.Sh...]
    reduce_scatter x1 -> x0, waiting for transfers between devices: 41.3 us -> none  [shards(): lax.psum_scatter(partial_sum, 'row', scatter_dimension=0, tiled=True)]
    all_gather x1 -> x0, waiting for transfers between devices: 40.1 us -> none  [shards(): lax.all_gather(frontier, 'col', axis=0, tiled=True)]
    dynamic_slice x24 -> x0, local copies, waits for them, and re-layouts: 21 us -> none  [the longest x8 20.1 us: tile_product(): return lax.map(one_rows, row_blocks).reshape(row_total, vectors.shape[1])]
    dynamic_update_slice x4 -> x0, local copies, waits for them, and re-layouts: 3.37 us -> none  [tile_product(): return lax.map(one_rows, row_blocks).reshape(row_total, vectors.shape[1])]
  transfers between devices with their start and end apart: 2 -> 0, of which waited for: 2 -> 0; matrix products, arithmetic and copies ran while one was open for 0% -> 0% of each run, Pallas kernels for 0% -> 0%
where the time goes in v1:
time: 63.2 us; the launch traced here: 62.7 us
  Pallas kernels  56.6 us (90%)
  local copies, waits for them, and re-layouts  5.45 us (9%)
  between operations  0.64 us (1%)
    pallas_call x1, Pallas kernels, shards(): pl.pallas_call(functools.partial(kernel, n_row, n_col), out_shape=(jax.Sh...  56.6 us
    unnamed x2, local copies, waits for them, and re-layouts  3.19 us

profile of v1, /device:TPU:9, one launch (start us, length us, event | category | flops | bytes accessed | tf_op | source)
XLA Modules:
  0.0 62.7 jit_solution(8449884368482562784)
XLA Ops:
  0.6 1.2 %copy.7 = bf16[128,32,64]{0,2,1:T(8,128)(2,1)S(1)} copy(bf16[128,32,64]{0,1,2:T(8,128)(2,1)} %bitcast.5) | data formatting | bytes 1048576 | tf_op jit(solution)/shard_map/transpose | solution.py:243
  1.9 1.0 %copy.8.ft = bf16[128,2048]{1,0:T(8,128)(2,1)} copy(bf16[128,2048]{0,1:T(8,128)(2,1)S(1)} %bitcast.4) | data formatting | bytes 1048576 | tf_op jit(solution)/shard_map/reshape | solution.py:243
  2.9 56.6 %shard_map.50 = (f32[1024,128]{1,0:T(8,128)}, s32[4,1024]{1,0:T(4,128)}) custom-call(s32[4096,512]{1,0:T(8,128)} %adj.1, bf16[128,2048]{1,0:T(8,128)(2,1)} %copy.8.ft, s32[4,1024]{1,0:T(4,128)} %visited.1), custom_call_target="tpu_custom_call" | custom-call | tf_op jit(solution)/shard_map/pallas_call | solution.py:247
  59.5 1.9 %copy.11 = f32[1024,128]{1,0:T(8,128)} copy(f32[1024,128]{1,0:T(8,128)} %get-tuple-element.4) | data formatting | bytes 1048576
  61.4 1.3 %copy.12 = s32[4,1024]{1,0:T(4,128)} copy(s32[4,1024]{1,0:T(4,128)} %get-tuple-element.5) | data formatting | bytes 32768
